TPU v7x, 32 devices: a whole 2x2x4 slice. The times are simulated.
32 devices in a mesh: dp: 2 (over x), tp: 16 (over y, z, core).
Axes of the slice: x: 2, y: 2, z: 4, core: 2. Of those that a mesh axis runs over, the one named last changes fastest.
Arguments:
- x: bfloat16 [4096, 2048], P('dp'), parts along dimension 0
- w_gate: bfloat16 [2048, 16384], P(None, 'tp')
- w_up: bfloat16 [2048, 16384], P(None, 'tp')
- w_down: bfloat16 [16384, 2048], P('tp')
Outputs:
- output: bfloat16 [4096, 2048], P('dp'), parts along dimension 0
There are 2 independent parts. A program takes and returns all parts, laid end to end along the dimension named above; an argument that names none is the same for every part.
All inputs are finite; a program needn't handle non-finite values.
Results may differ from a plain program's by a relative error of at most 0.016.
Values are sent between devices in bfloat16 or wider.
A program may use at most 2 GiB of HBM per device.

v0:
```python
import jax
import jax.numpy as jnp
from jax import lax
from jax.sharding import PartitionSpec as P


def solution(mesh):
    def step(x, w_gate, w_up, w_down):
        gate = jnp.dot(x, w_gate, preferred_element_type=jnp.float32)
        up = jnp.dot(x, w_up, preferred_element_type=jnp.float32)
        hidden = (jax.nn.gelu(gate) * up).astype(jnp.bfloat16)
        term = jnp.dot(hidden, w_down, preferred_element_type=jnp.float32).astype(jnp.bfloat16)
        return lax.psum(term, "tp")

    return jax.shard_map(
        step,
        mesh=mesh,
        in_specs=(P("dp", None), P(None, "tp"), P(None, "tp"), P("tp", None)),
        out_specs=P("dp", None),
        check_vma=False,
    )
```

profile of v0, /device:TPU:0, one launch (start us, length us, event | category | flops | bytes accessed | tf_op | source)
XLA Modules:
  0.0 235.6 jit_solution(13221919974002981891)
XLA Ops:
  6.5 0.0 all-reduce.2.cloned.1.call-start
  6.5 14.5 %fusion.17 = f32[2048,1024]{1,0:T(8,128)} fusion(bf16[2048,2048]{1,0:T(8,128)(2,1)} %param.4, bf16[2048,1024]{1,0:T(8,128)(2,1)} %param.5), kind=kOutput, calls=%fused_computation.19 | convolution fusion | flops 8589934592 | bytes 20971520 | tf_op jit(solution)/shard_map/dot_general | solution.py:9
  21.0 26.6 %convolution_convert_fusion = bf16[2048,2048]{1,0:T(8,128)(2,1)} fusion(bf16[1024,2048]{1,0:T(8,128)(2,1)} %param.7, f32[2048,1024]{1,0:T(8,128)} %fusion.17, bf16[2048,2048]{1,0:T(8,128)(2,1)} %param.4, bf16[2048,1024]{1,0:T(8,128)(2,1)} %param.6), kind=kOutput, calls=%fused_computation.10 | convolution fusion | flops 17205035008 | bytes 33554432 | tf_op jit(solution)/shard_map/dot_general | solution.py:12
  47.6 0.0 all-reduce.2.cloned.1.call-update
  47.7 172.6 %all-reduce.2.cloned.1.call-done = bf16[2048,2048]{1,0:T(8,128)(2,1)} async-done(((bf16[2048,2048]{1,0:T(8,128)(2,1)}), bf16[2048,2048]{1,0:T(8,128)(2,1)}) %all-reduce.2.cloned.1.call-update) | async-done | bytes 8388624 | tf_op jit(solution)/shard_map/psum | solution.py:13
  220.3 8.4 %copy.6 = bf16[2048,2048]{1,0:T(8,128)(2,1)} copy(bf16[2048,2048]{1,0:T(8,128)(2,1)} %all-reduce.2.cloned.1.call-done) | data formatting | bytes 16777216
Async XLA Ops:
  6.5 213.8 %all-reduce.2.cloned.1.call-start = ((), (), s32[]{:S(2)}) async-start(), calls=%async_computation | async-start | bytes 16777216 | tf_op jit(solution)/shard_map/psum | solution.py:13
Sparse Core Ops, SparseCore 0:
  47.8 172.4 all-reduce.1
where the time goes:
time: 236 us
  waiting for transfers between devices  173 us (73%)
  matrix products  41.1 us (17%)
  between operations  13.4 us (6%)
  local copies, waits for them, and re-layouts  8.44 us (4%)
    psum x1, waiting for transfers between devices, step(): return lax.psum(term, 'tp')  173 us
    dot_general x1, matrix products, step(): jnp.dot(hidden, w_down, preferred_element_type=jnp.float32)  26.6 us
    dot_general x1, matrix products, step(): gate = jnp.dot(x, w_gate, preferred_element_type=jnp.float32)  14.5 us
    unnamed x1, local copies, waits for them, and re-layouts  8.44 us
  transfers between devices with their start and end apart: 1, of which 1 were waited for; matrix products, arithmetic and copies ran while one was open for 0% of the time, Pallas kernels for 0%

commit v1 on v0

v1 whole, which is shorter than its diff:
```python
import functools

import jax
import jax.numpy as jnp
from jax import lax
from jax.experimental import pallas as pl
from jax.experimental.pallas import tpu as pltpu
from jax.sharding import PartitionSpec as P

F32, BF16 = jnp.float32, jnp.bfloat16

R = 256
R1, R2 = 160, 96
ROOT1 = (0, 3)
ROOT2 = (0, 1, 2, 3)
NZ = 4


def _lag(z, k):
    return jnp.where(z < k, z, jnp.where(z > k, NZ - 1 - z, max(k, NZ - 1 - k)))


def kernel(
    x_hbm, wg_hbm, wu_hbm, wd_hbm, y,
    x, wg, wu, wd, hid, part,
    sy1, ry1, sz1, rl1, rr1, sz2, rl2, rr2, sy2, ry2,
    in_sem, wd_s, wd_r, hid_s, hid_r,
    y1_s, y1_r, z1_s, l1_r, r1_r, bl1_s, br1_s, b1_r, a1_s, a1_r,
    z2_s, l2_r, r2_r, y2_s, y2_r, a2_s, a2_r, bl2_s, br2_s, b2_r,
    df_s, df_r,
):
    rows, width = y.shape
    n_super = rows // R
    n = 2 * n_super
    half = width // 2
    cw = half // 2
    units = wg_hbm.shape[1]
    uh = units // 2
    n1, n2 = len(ROOT1), len(ROOT2)
    w1 = cw // 2 // n1
    w2 = cw // n2
    rh = R2 // 2

    me = lax.axis_index("tp")
    core = lax.rem(me, 2)
    z = lax.rem(lax.div(me, 2), NZ)
    yy = lax.div(me, 2 * NZ)
    peer = {"tp": me + 1 - 2 * core}
    ypeer = {"tp": lax.rem(me + 2 * NZ, 4 * NZ)}
    left = {"tp": me - 2}
    right = {"tp": me + 2}

    def load(i, src, dst):
        return pltpu.make_async_copy(src, dst, in_sem.at[i])

    def al(v, m):
        return pl.multiple_of(v, m)

    def x_copy(s):
        return load(s, x_hbm.at[pl.ds(al(s * R, R), R)], x.at[s])

    def g_copy(j):
        return load(n_super + j, wg_hbm.at[:, pl.ds(j * uh, uh)], wg.at[j])

    def u_copy(j):
        return load(n_super + 2 + j, wu_hbm.at[:, pl.ds(j * uh, uh)], wu.at[j])

    def d_copy(j):
        return load(
            n_super + 4 + j,
            wd_hbm.at[:, pl.ds(al(core * half + j * cw, cw), cw)],
            wd.at[j, pl.ds(al(core * units, units), units)],
        )

    def remote(src, dst, ssem, rsem, dev):
        return pltpu.make_async_remote_copy(
            src_ref=src, dst_ref=dst, send_sem=ssem, recv_sem=rsem,
            device_id=dev, device_id_type=pl.DeviceIdType.MESH,
        )

    x_copy(0).start()
    g_copy(0).start()
    u_copy(0).start()
    g_copy(1).start()
    u_copy(1).start()
    if n_super > 1:
        x_copy(1).start()
    d_copy(0).start()
    d_copy(1).start()

    barrier = pltpu.get_barrier_semaphore()

    def hello(dev):
        pl.semaphore_signal(barrier, inc=1, device_id=dev, device_id_type=pl.DeviceIdType.MESH)

    hello(peer)
    hello(ypeer)
    pl.when(z > 0)(lambda: hello(left))
    pl.when(z < NZ - 1)(lambda: hello(right))
    pl.semaphore_wait(barrier, 2 + jnp.minimum(z, 1) + jnp.minimum(NZ - 1 - z, 1))

    def wd_msg(j):
        return remote(
            wd_hbm.at[:, pl.ds(al((1 - core) * half + j * cw, cw), cw)],
            wd.at[j, pl.ds(al(core * units, units), units)],
            wd_s.at[j], wd_r.at[j], peer,
        )

    wd_msg(0).start()
    wd_msg(1).start()
    for s in range(2, n_super):
        x_copy(s).start()

    def hid_msg(c):
        s, j = lax.div(c, 2), lax.rem(c, 2)
        place = hid.at[s, :, pl.ds(al(core * units + j * uh, uh), uh)]
        return remote(place, place, hid_s.at[c], hid_r.at[c], peer)

    def row0(c):
        return al(lax.div(c, 2) * R, R)

    def col0(c, who):
        return al(who * half + lax.rem(c, 2) * cw, cw)

    def y1_place(c, h, p):
        return y.at[pl.ds(row0(c), R1), pl.ds(al(col0(c, core) + h * (cw // 2) + p * w1, w1), w1)]

    def y2_place(c, q):
        return y.at[pl.ds(al(row0(c) + R1, 16), R2), pl.ds(al(col0(c, core) + q * w2, w2), w2)]

    def y2_rows(c, q, h):
        return y.at[pl.ds(al(row0(c) + R1 + h * rh, 16), rh), pl.ds(al(col0(c, core) + q * w2, w2), w2)]

    def part1(c, h, p):
        return part.at[c, pl.ds(0, R1), pl.ds(al(h * (cw // 2) + p * w1, w1), w1)]

    def part2(c, q):
        return part.at[c, pl.ds(R1, R2), pl.ds(q * w2, w2)]

    def part2_rows(c, q, h):
        return part.at[c, pl.ds(al(R1 + h * rh, 16), rh), pl.ds(q * w2, w2)]

    def m_y1(c, p):
        return remote(sy1.at[c, p], ry1.at[c, p], y1_s.at[c, p], y1_r.at[c, p], ypeer)

    def m_z1(c, p, to_right):
        dst, sem = (rl1, l1_r) if to_right else (rr1, r1_r)
        return remote(sz1.at[c, p], dst.at[c, p], z1_s.at[c, p], sem.at[c, p], right if to_right else left)

    def m_b1(c, p, to_right):
        place = y1_place(c, yy, p)
        return remote(place, place, (br1_s if to_right else bl1_s).at[c, p], b1_r.at[c, p], right if to_right else left)

    def m_a1(c, p, h):
        place = y1_place(c, h, p)
        return remote(place, place, a1_s.at[c, p], a1_r.at[c, p], ypeer)

    def m_z2(c, q, to_right):
        dst, sem = (rl2, l2_r) if to_right else (rr2, r2_r)
        return remote(sz2.at[c, q], dst.at[c, q], z2_s.at[c, q], sem.at[c, q], right if to_right else left)

    def m_y2(c, q):
        return remote(sy2.at[c], ry2.at[c], y2_s.at[c, q], y2_r.at[c, q], ypeer)

    def m_a2(c, q, h):
        place = y2_rows(c, q, h)
        return remote(place, place, a2_s.at[c, q], a2_r.at[c, q], ypeer)

    def m_b2(c, q, to_right):
        place = y2_place(c, q)
        return remote(place, place, (br2_s if to_right else bl2_s).at[c, q], b2_r.at[c, q], right if to_right else left)

    def m_df(c, who):
        place = y.at[pl.ds(row0(c), R), pl.ds(col0(c, who), cw)]
        return remote(place, place, df_s.at[c], df_r.at[c], peer)

    def gate_up(it):
        s, j = lax.div(it, 2), lax.rem(it, 2)

        @pl.when(j == 0)
        def _():
            x_copy(s).wait()

        @pl.when(it == 0)
        def _():
            g_copy(0).wait()
            u_copy(0).wait()

        @pl.when(it == 1)
        def _():
            g_copy(1).wait()
            u_copy(1).wait()

        nb = min(256, uh)
        for b in range(uh // nb):
            cols = pl.ds(b * nb, nb)
            gate = jnp.dot(x[s], wg[j, :, cols], preferred_element_type=F32)
            up = jnp.dot(x[s], wu[j, :, cols], preferred_element_type=F32)
            hid[s, :, pl.ds(al(core * units + j * uh + b * nb, nb), nb)] = (jax.nn.gelu(gate) * up).astype(BF16)
        hid_msg(it).start()

    def down(c):
        s, j = lax.div(c, 2), lax.rem(c, 2)

        @pl.when(c == 0)
        def _():
            d_copy(0).wait()
            wd_msg(0).wait_recv()

        @pl.when(c == 1)
        def _():
            d_copy(1).wait()
            wd_msg(1).wait_recv()

        @pl.when(j == 0)
        def _():
            hid_msg(c).wait_recv()
            hid_msg(c + 1).wait_recv()

        nb = 256
        for b in range(cw // nb):
            cols = pl.ds(b * nb, nb)
            part[c, :, cols] = jnp.dot(hid[s], wd[j, :, cols], preferred_element_type=F32)
        for p in range(n1):
            sy1[c, p] = part1(c, 1 - yy, p)[...].astype(BF16)
            m_y1(c, p).start()

    def guarded(c, f):
        pl.when((c >= 0) & (c < n))(lambda: f(c))

    def chain(c, k, acc, lbuf, rbuf, sbuf, msg, root):
        @pl.when((z >= 1) & (z <= k))
        def _():
            msg(True).wait_recv()
            acc[...] += lbuf[...].astype(F32)

        @pl.when((z <= NZ - 2) & (z >= k))
        def _():
            msg(False).wait_recv()
            acc[...] += rbuf[...].astype(F32)

        @pl.when(z != k)
        def _():
            sbuf[...] = acc[...].astype(BF16)
            pl.when(z < k)(lambda: msg(True).start())
            pl.when(z > k)(lambda: msg(False).start())

        pl.when(z == k)(root)

    def spread(k, msg):
        if k < NZ - 1:
            pl.when((z >= k) & (z < NZ - 1))(lambda: msg(True).start())
        if k > 0:
            pl.when((z <= k) & (z > 0))(lambda: msg(False).start())

    def reduce1(c, p):
        k = ROOT1[p]
        acc = part1(c, yy, p)
        m_y1(c, p).wait_recv()
        acc[...] += ry1[c, p].astype(F32)

        def root():
            y1_place(c, yy, p)[...] = acc[...].astype(BF16)
            spread(k, lambda to_right: m_b1(c, p, to_right))
            m_a1(c, p, yy).start()

        chain(c, k, acc, rl1.at[c, p], rr1.at[c, p], sz1.at[c, p], lambda to_right: m_z1(c, p, to_right), root)

    def bcast1(c, p):
        k = ROOT1[p]

        @pl.when(z != k)
        def _():
            m_b1(c, p, True).wait_recv()
            spread(k, lambda to_right: m_b1(c, p, to_right))
            m_a1(c, p, yy).start()

    def reduce2(c, q):
        k = ROOT2[q]
        acc = part2(c, q)

        def root():
            sy2[c] = part2_rows(c, q, 1 - yy)[...].astype(BF16)
            m_y2(c, q).start()

        chain(c, k, acc, rl2.at[c, q], rr2.at[c, q], sz2.at[c, q], lambda to_right: m_z2(c, q, to_right), root)

    def cross2(c, q):
        @pl.when(z == ROOT2[q])
        def _():
            m_y2(c, q).wait_recv()
            y2_rows(c, q, yy)[...] = (part2_rows(c, q, yy)[...] + ry2[c].astype(F32)).astype(BF16)
            m_a2(c, q, yy).start()

    def bcast2(c, q):
        k = ROOT2[q]
        pl.when(z == k)(lambda: m_a2(c, q, 1 - yy).wait_recv())
        pl.when(z != k)(lambda: m_b2(c, q, True).wait_recv())
        spread(k, lambda to_right: m_b2(c, q, to_right))

    def finish(c):
        for p in range(n1):
            m_a1(c, p, 1 - yy).wait_recv()
        m_df(c, core).start()

    def dist(k):
        return jnp.where(z < k, k - z, z - k)

    last = max(
        [3 + max(k, NZ - 1 - k) * 2 + 1 for k in ROOT1] + [4 + max(k, NZ - 1 - k) * 2 for k in ROOT2]
    )

    def step(it, carry):
        pl.when(it < n)(lambda: gate_up(it))
        guarded(it - 2, down)
        for p in range(n1):
            guarded(it - 3 - _lag(z, ROOT1[p]), functools.partial(reduce1, p=p))
        for q in range(n2):
            guarded(it - 2 - _lag(z, ROOT2[q]), functools.partial(reduce2, q=q))
        for q, k in enumerate(ROOT2):
            guarded(it - 3 - max(k, NZ - 1 - k), functools.partial(cross2, q=q))
        for p, k in enumerate(ROOT1):
            guarded(it - 3 - max(k, NZ - 1 - k) - dist(k), functools.partial(bcast1, p=p))
        for q, k in enumerate(ROOT2):
            guarded(it - 4 - max(k, NZ - 1 - k) - dist(k), functools.partial(bcast2, q=q))
        guarded(it - last, finish)
        return carry

    lax.fori_loop(0, n + last, step, 0)

    wd_msg(0).wait_send()
    wd_msg(1).wait_send()

    def drain(c, carry):
        hid_msg(c).wait_send()
        for p, k in enumerate(ROOT1):
            m_y1(c, p).wait_send()
            pl.when(z != k)(lambda: m_z1(c, p, True).wait_send())
            if k < NZ - 1:
                pl.when((z >= k) & (z < NZ - 1))(lambda: m_b1(c, p, True).wait_send())
            if k > 0:
                pl.when((z <= k) & (z > 0))(lambda: m_b1(c, p, False).wait_send())
            m_a1(c, p, yy).wait_send()
        for q, k in enumerate(ROOT2):
            pl.when(z != k)(lambda: m_z2(c, q, True).wait_send())

            @pl.when(z == k)
            def _():
                m_y2(c, q).wait_send()
                m_a2(c, q, yy).wait_send()

            if k < NZ - 1:
                pl.when((z >= k) & (z < NZ - 1))(lambda: m_b2(c, q, True).wait_send())
            if k > 0:
                pl.when((z <= k) & (z > 0))(lambda: m_b2(c, q, False).wait_send())
        m_df(c, core).wait_send()
        m_df(c, 1 - core).wait_recv()
        return carry

    lax.fori_loop(0, n, drain, 0)


def block(x, w_gate, w_up, w_down):
    rows, width = x.shape
    units = w_gate.shape[1]
    n_super = rows // R
    n = 2 * n_super
    cw = width // 4
    n1, n2 = len(ROOT1), len(ROOT2)
    w1, w2 = cw // 2 // n1, cw // n2
    dma = pltpu.SemaphoreType.DMA
    one = pltpu.VMEM((n, n1, R1, w1), BF16)
    two = pltpu.VMEM((n, n2, R2, w2), BF16)
    cross = pltpu.VMEM((n, R2 // 2, w2), BF16)
    return pl.pallas_call(
        kernel,
        out_shape=pltpu.VMEM((rows, width), BF16),
        in_specs=[pl.BlockSpec(memory_space=pl.ANY)] * 4,
        out_specs=pl.BlockSpec(memory_space=pltpu.VMEM),
        scratch_shapes=[
            pltpu.VMEM((n_super, R, width), BF16),
            pltpu.VMEM((2, width, units // 2), BF16),
            pltpu.VMEM((2, width, units // 2), BF16),
            pltpu.VMEM((2, 2 * units, cw), BF16),
            pltpu.VMEM((n_super, R, 2 * units), BF16),
            pltpu.VMEM((n, R, cw), F32),
            one, one, one, one, one, two, two, two, cross, cross,
            dma((n_super + 6,)), dma((2,)), dma((2,)), dma((n,)), dma((n,)),
            *[dma((n, n1))] * 10,
            *[dma((n, n2))] * 10,
            dma((n,)), dma((n,)),
        ],
        compiler_params=pltpu.CompilerParams(
            collective_id=0, has_side_effects=True, vmem_limit_bytes=52 * 1024 * 1024
        ),
    )(x, w_gate, w_up, w_down)


def solution(mesh):
    return jax.shard_map(
        block,
        mesh=mesh,
        in_specs=(P("dp", None), P(None, "tp"), P(None, "tp"), P("tp", None)),
        out_specs=P("dp", None),
        check_vma=False,
    )
```

time: 236 us -> 112 us (0.47)
  waiting for transfers between devices: 173 us -> 0 us
  Pallas kernels: 0 us -> 108 us
  matrix products: 41.1 us -> 0 us
  between operations: 13.4 us -> 0.01 us
  local copies, waits for them, and re-layouts: 8.44 us -> 3.4 us
    psum x1 -> x0, waiting for transfers between devices: 173 us -> none  [step(): return lax.psum(term, 'tp')]
    pallas_call x0 -> x1, Pallas kernels: none -> 108 us  [block(): pl.pallas_call(kernel, out_shape=pltpu.VMEM((rows, width), BF16), in_spec...]
    dot_general x2 -> x0, matrix products: 41.1 us -> none  [the longest x1 26.6 us: step(): jnp.dot(hidden, w_down, preferred_element_type=jnp.float32)]
    unnamed x1, local copies, waits for them, and re-layouts: 8.44 us -> 3.4 us
  transfers between devices with their start and end apart: 1 -> 0, of which waited for: 1 -> 0; matrix products, arithmetic and copies ran while one was open for 0% -> 0% of each run, Pallas kernels for 0% -> 0%
where the time goes in v1:
time: 112 us; the launch traced here: 111 us
  Pallas kernels  108 us (96%)
  local copies, waits for them, and re-layouts  3.4 us (3%)
    pallas_call x1, Pallas kernels, block(): pl.pallas_call(kernel, out_shape=pltpu.VMEM((rows, width), BF16), in_spec...  108 us
    unnamed x1, local copies, waits for them, and re-layouts  3.4 us

profile of v1, /device:TPU:0, one launch (start us, length us, event | category | flops | bytes accessed | tf_op | source)
XLA Modules:
  0.0 111.5 jit_solution(13709690379443643287)
XLA Ops:
  0.0 108.1 %shard_map.46 = bf16[2048,2048]{1,0:T(8,128)(2,1)S(1)} custom-call(bf16[2048,2048]{1,0:T(8,128)(2,1)} %x_hbm.1, bf16[2048,1024]{1,0:T(8,128)(2,1)} %wg_hbm.1, bf16[2048,1024]{1,0:T(8,128)(2,1)} %wu_hbm.1, bf16[1024,2048]{1,0:T(8,128)(2,1)} %wd_hbm.1), custom_call_target="tpu_custom_call" | custom-call | tf_op jit(solution)/shard_map/pallas_call | solution.py:375
  108.1 3.4 %copy.6 = bf16[2048,2048]{1,0:T(8,128)(2,1)} copy(bf16[2048,2048]{1,0:T(8,128)(2,1)S(1)} %shard_map.46) | data formatting | bytes 16777216

commit v2 on v1

v2 whole, which is shorter than its diff:
```python
import functools

import jax
import jax.numpy as jnp
from jax import lax
from jax.experimental import pallas as pl
from jax.experimental.pallas import tpu as pltpu
from jax.sharding import PartitionSpec as P

F32, BF16 = jnp.float32, jnp.bfloat16

R = 256
R1, R2 = 192, 64
NJ = 2
ROOT1 = (0, 3)
ROOT2 = (0, 3, 1, 2)
M1, M2 = 1, 1
NZ = 4
HY, HZ, HX, HB, EB, HF = 2, 2, 2, 2, 1, 0


def _far(k):
    return max(k, NZ - 1 - k)


def _hops(z, k):
    return jnp.where(z < k, z, jnp.where(z > k, NZ - 1 - z, _far(k)))


def kernel(
    x_hbm, wg_hbm, wu_hbm, wd_hbm, y,
    x, wg, wu, wd, hid, part,
    sy1, ry1, sz1, rl1, rr1, sz2, rl2, rr2, sy2, ry2,
    in_sem, wd_s, wd_r, hid_s, hid_r,
    y1_s, y1_r, z1_s, l1_r, r1_r, bl1_s, br1_s, b1_r, a1_s, a1_r,
    z2_s, l2_r, r2_r, y2_s, y2_r, a2_s, a2_r, bl2_s, br2_s, b2_r,
    df_s, df_r,
):
    rows, width = y.shape
    n_super = rows // R
    n = NJ * n_super
    half = width // 2
    cw = half // NJ
    units = wg_hbm.shape[1]
    uh = units // NJ
    nb = min(256, uh)
    blocks = units // nb
    w1 = cw // 2 * M1 // len(ROOT1)
    w2 = cw * M2 // len(ROOT2)

    me = lax.axis_index("tp")
    core = lax.rem(me, 2)
    z = lax.rem(lax.div(me, 2), NZ)
    yy = lax.div(me, 2 * NZ)
    peer = {"tp": me + 1 - 2 * core}
    ypeer = {"tp": lax.rem(me + 2 * NZ, 4 * NZ)}
    left = {"tp": me - 2}
    right = {"tp": me + 2}

    def load(i, src, dst):
        return pltpu.make_async_copy(src, dst, in_sem.at[i])

    def al(v, m):
        return pl.multiple_of(v, m)

    def x_copy(s):
        return load(s, x_hbm.at[pl.ds(al(s * R, R), R)], x.at[s])

    def g_copy(b):
        return load(n_super + b, wg_hbm.at[:, pl.ds(b * nb, nb)], wg.at[b])

    def u_copy(b):
        return load(n_super + blocks + b, wu_hbm.at[:, pl.ds(b * nb, nb)], wu.at[b])

    def d_copy(j):
        return load(
            n_super + 2 * blocks + j,
            wd_hbm.at[:, pl.ds(al(core * half + j * cw, cw), cw)],
            wd.at[j, pl.ds(al(core * units, units), units)],
        )

    def remote(src, dst, ssem, rsem, dev):
        return pltpu.make_async_remote_copy(
            src_ref=src, dst_ref=dst, send_sem=ssem, recv_sem=rsem,
            device_id=dev, device_id_type=pl.DeviceIdType.MESH,
        )

    x_copy(0).start()
    for b in range(blocks):
        g_copy(b).start()
        u_copy(b).start()
    for j in range(NJ):
        d_copy(j).start()
    x_copy(1).start()

    barrier = pltpu.get_barrier_semaphore()

    def hello(dev):
        pl.semaphore_signal(barrier, inc=1, device_id=dev, device_id_type=pl.DeviceIdType.MESH)

    hello(peer)
    hello(ypeer)
    pl.when(z > 0)(lambda: hello(left))
    pl.when(z < NZ - 1)(lambda: hello(right))
    pl.semaphore_wait(barrier, 2 + jnp.minimum(z, 1) + jnp.minimum(NZ - 1 - z, 1))

    def wd_msg(j):
        return remote(
            wd_hbm.at[:, pl.ds(al((1 - core) * half + j * cw, cw), cw)],
            wd.at[j, pl.ds(al(core * units, units), units)],
            wd_s.at[j], wd_r.at[j], peer,
        )

    for j in range(NJ):
        wd_msg(j).start()
    for s in range(2, n_super):
        x_copy(s).start()

    def hid_msg(c):
        s, j = lax.div(c, NJ), lax.rem(c, NJ)
        place = hid.at[s, :, pl.ds(al(core * units + j * uh, uh), uh)]
        return remote(place, place, hid_s.at[c], hid_r.at[c], peer)

    def row0(c):
        return al(lax.div(c, NJ) * R, R)

    def col0(c, who):
        return al(who * half + lax.rem(c, NJ) * cw, cw)

    def y1_place(c, h, p):
        return y.at[pl.ds(row0(c), R1), pl.ds(al(col0(c, core) + h * (cw // 2) + p // M1 * w1, w1), w1)]

    def y2_place(c, q):
        return y.at[pl.ds(al(row0(c) + R1, 16), R2), pl.ds(al(col0(c, core) + q // M2 * w2, w2), w2)]

    def part1(c, h, p):
        return part.at[c, pl.ds(0, R1), pl.ds(al(h * (cw // 2) + p // M1 * w1, w1), w1)]

    def part2(c, q):
        return part.at[c, pl.ds(R1, R2), pl.ds(q // M2 * w2, w2)]

    def m_y1(c, p):
        i = p // M1
        return remote(sy1.at[c, i], ry1.at[c, i], y1_s.at[c, i], y1_r.at[c, i], ypeer)

    def m_z1(c, p, to_right):
        i = p // M1
        dst, sem = (rl1, l1_r) if to_right else (rr1, r1_r)
        return remote(sz1.at[c, i], dst.at[c, i], z1_s.at[c, i], sem.at[c, i], right if to_right else left)

    def m_b1(c, p, to_right):
        i = p // M1
        place = y1_place(c, yy, p)
        return remote(place, place, (br1_s if to_right else bl1_s).at[c, i], b1_r.at[c, i], right if to_right else left)

    def m_a1(c, p, h):
        i = p // M1
        place = y1_place(c, h, p)
        return remote(place, place, a1_s.at[c, i], a1_r.at[c, i], ypeer)

    def m_z2(c, q, to_right):
        i = q // M2
        dst, sem = (rl2, l2_r) if to_right else (rr2, r2_r)
        return remote(sz2.at[c, i], dst.at[c, i], z2_s.at[c, i], sem.at[c, i], right if to_right else left)

    def m_y2(c, q):
        return remote(sy2.at[c], ry2.at[c], y2_s.at[c], y2_r.at[c], ypeer)

    def m_a2(c, q):
        place = y2_place(c, q)
        return remote(place, place, a2_s.at[c], a2_r.at[c], ypeer)

    def m_b2(c, q, to_right):
        i = q // M2
        place = y2_place(c, q)
        return remote(place, place, (br2_s if to_right else bl2_s).at[c, i], b2_r.at[c, i], right if to_right else left)

    def y_root(c, q):
        return lax.rem(lax.div(c, M2) + q // 2, 2) == yy

    def m_df(c, who):
        place = y.at[pl.ds(row0(c), R), pl.ds(col0(c, who), cw)]
        return remote(place, place, df_s.at[c], df_r.at[c], peer)

    def gate_up_wait(it):
        @pl.when(lax.rem(it, NJ) == 0)
        def _():
            x_copy(lax.div(it, NJ)).wait()

    def gate_up(it, first=None):
        s, j = lax.div(it, NJ), lax.rem(it, NJ)
        for b in range(uh // nb):
            block = j * (uh // nb) + b
            if first is not None:
                g_copy(first * (uh // nb) + b).wait()
                u_copy(first * (uh // nb) + b).wait()
            gate = jnp.dot(x[s], wg[block], preferred_element_type=F32)
            up = jnp.dot(x[s], wu[block], preferred_element_type=F32)
            hid[s, :, pl.ds(al(core * units + j * uh + b * nb, nb), nb)] = (jax.nn.gelu(gate) * up).astype(BF16)

    def down_wait(c):
        for j in range(NJ):

            @pl.when(c == j)
            def _():
                d_copy(j).wait()
                wd_msg(j).wait_recv()

        @pl.when(lax.rem(c, NJ) == 0)
        def _():
            for j in range(NJ):
                hid_msg(c + j).wait_recv()

    def down(c):
        s, j = lax.div(c, NJ), lax.rem(c, NJ)
        db = min(256, cw)
        for b in range(cw // db):
            cols = pl.ds(b * db, db)
            part[c, :, cols] = jnp.dot(hid[s], wd[j, :, cols], preferred_element_type=F32)

    def down_send(c):
        for p in range(len(ROOT1)):

            @pl.when(active(c, p, M1))
            def _():
                sy1[c, p // M1] = part1(c, 1 - yy, p)[...].astype(BF16)
                m_y1(c, p).start()

    def compute(it):
        for j in range(NJ):

            @pl.when(it == j)
            def _():
                gate_up_wait(it)
                gate_up(it, first=j)
                hid_msg(it).start()

        @pl.when((it >= NJ) & (it < n))
        def _():
            gate_up_wait(it)
            down_wait(it - NJ)
            gate_up(it)
            down(it - NJ)
            hid_msg(it).start()
            down_send(it - NJ)

        @pl.when((it >= n) & (it < n + NJ))
        def _():
            down_wait(it - NJ)
            down(it - NJ)
            down_send(it - NJ)

    def active(c, p, m):
        return True if m == 1 else lax.rem(c, m) == p % m

    def guarded(c, f, p=0, m=1):
        pl.when((c >= 0) & (c < n) & active(c, p, m))(lambda: f(c))

    def chain(c, k, acc, lbuf, rbuf, sbuf, msg, root):
        @pl.when((z >= 1) & (z <= k))
        def _():
            msg(True).wait_recv()
            acc[...] += lbuf[...].astype(F32)

        @pl.when((z <= NZ - 2) & (z >= k))
        def _():
            msg(False).wait_recv()
            acc[...] += rbuf[...].astype(F32)

        @pl.when(z != k)
        def _():
            sbuf[...] = acc[...].astype(BF16)
            pl.when(z < k)(lambda: msg(True).start())
            pl.when(z > k)(lambda: msg(False).start())

        pl.when(z == k)(root)

    def spread(k, msg):
        if k < NZ - 1:
            pl.when((z >= k) & (z < NZ - 1))(lambda: msg(True).start())
        if k > 0:
            pl.when((z <= k) & (z > 0))(lambda: msg(False).start())

    def reduce1(c, p):
        k = ROOT1[p]
        i = p // M1
        acc = part1(c, yy, p)
        m_y1(c, p).wait_recv()
        acc[...] += ry1[c, i].astype(F32)

        def root():
            y1_place(c, yy, p)[...] = acc[...].astype(BF16)
            spread(k, lambda to_right: m_b1(c, p, to_right))
            m_a1(c, p, yy).start()

        chain(c, k, acc, rl1.at[c, i], rr1.at[c, i], sz1.at[c, i], lambda to_right: m_z1(c, p, to_right), root)

    def bcast1(c, p):
        k = ROOT1[p]

        @pl.when(z != k)
        def _():
            m_b1(c, p, True).wait_recv()
            spread(k, lambda to_right: m_b1(c, p, to_right))
            m_a1(c, p, yy).start()

    def reduce2(c, q):
        k = ROOT2[q]
        i = q // M2
        acc = part2(c, q)

        def root():
            @pl.when(jnp.logical_not(y_root(c, q)))
            def _():
                sy2[c] = acc[...].astype(BF16)
                m_y2(c, q).start()

        chain(c, k, acc, rl2.at[c, i], rr2.at[c, i], sz2.at[c, i], lambda to_right: m_z2(c, q, to_right), root)

    def cross2(c, q):
        @pl.when((z == ROOT2[q]) & y_root(c, q))
        def _():
            m_y2(c, q).wait_recv()
            y2_place(c, q)[...] = (part2(c, q)[...] + ry2[c].astype(F32)).astype(BF16)
            m_a2(c, q).start()

    def bcast2(c, q):
        k = ROOT2[q]
        pl.when((z == k) & jnp.logical_not(y_root(c, q)))(lambda: m_a2(c, q).wait_recv())
        pl.when(z != k)(lambda: m_b2(c, q, True).wait_recv())
        spread(k, lambda to_right: m_b2(c, q, to_right))

    def finish(c):
        for p in range(len(ROOT1)):
            pl.when(active(c, p, M1))(lambda: m_a1(c, p, 1 - yy).wait_recv())
        m_df(c, core).start()

    def dist(k):
        return jnp.where(z < k, k - z, z - k)

    last = max(
        [NJ + HY + EB + HF + (HZ + HB) * _far(k) for k in ROOT1]
        + [NJ + 2 * HX + EB + (HZ + HB) * _far(k) for k in ROOT2]
    )

    def step(it, carry):
        compute(it)
        for p, k in enumerate(ROOT1):
            guarded(it - (NJ + HY) - HZ * _hops(z, k), functools.partial(reduce1, p=p), p, M1)
        for q, k in enumerate(ROOT2):
            guarded(it - NJ - HZ * _hops(z, k), functools.partial(reduce2, q=q), q, M2)
        for q, k in enumerate(ROOT2):
            guarded(it - (NJ + HX) - HZ * _far(k), functools.partial(cross2, q=q), q, M2)
        for p, k in enumerate(ROOT1):
            guarded(it - (NJ + HY + EB) - HZ * _far(k) - HB * dist(k), functools.partial(bcast1, p=p), p, M1)
        for q, k in enumerate(ROOT2):
            guarded(it - (NJ + 2 * HX + EB) - HZ * _far(k) - HB * dist(k), functools.partial(bcast2, q=q), q, M2)
        guarded(it - last, finish)
        return carry

    lax.fori_loop(0, n + last, step, 0)

    for j in range(NJ):
        wd_msg(j).wait_send()

    def drain(c, carry):
        hid_msg(c).wait_send()
        for p, k in enumerate(ROOT1):

            @pl.when(active(c, p, M1))
            def _():
                m_y1(c, p).wait_send()
                pl.when(z != k)(lambda: m_z1(c, p, True).wait_send())
                if k < NZ - 1:
                    pl.when((z >= k) & (z < NZ - 1))(lambda: m_b1(c, p, True).wait_send())
                if k > 0:
                    pl.when((z <= k) & (z > 0))(lambda: m_b1(c, p, False).wait_send())
                m_a1(c, p, yy).wait_send()

        for q, k in enumerate(ROOT2):

            @pl.when(active(c, q, M2))
            def _():
                pl.when(z != k)(lambda: m_z2(c, q, True).wait_send())
                pl.when((z == k) & jnp.logical_not(y_root(c, q)))(lambda: m_y2(c, q).wait_send())
                pl.when((z == k) & y_root(c, q))(lambda: m_a2(c, q).wait_send())
                if k < NZ - 1:
                    pl.when((z >= k) & (z < NZ - 1))(lambda: m_b2(c, q, True).wait_send())
                if k > 0:
                    pl.when((z <= k) & (z > 0))(lambda: m_b2(c, q, False).wait_send())

        m_df(c, core).wait_send()
        m_df(c, 1 - core).wait_recv()
        return carry

    lax.fori_loop(0, n, drain, 0)


def block(x, w_gate, w_up, w_down):
    rows, width = x.shape
    units = w_gate.shape[1]
    n_super = rows // R
    n = NJ * n_super
    cw = width // 2 // NJ
    n1, n2 = len(ROOT1) // M1, len(ROOT2) // M2
    w1, w2 = cw // 2 // n1, cw // n2
    nb = min(256, units // NJ)
    blocks = units // nb
    dma = pltpu.SemaphoreType.DMA
    one = pltpu.VMEM((n, n1, R1, w1), BF16)
    two = pltpu.VMEM((n, n2, R2, w2), BF16)
    cross = pltpu.VMEM((n, R2, w2), BF16)
    return pl.pallas_call(
        kernel,
        out_shape=pltpu.VMEM((rows, width), BF16),
        in_specs=[pl.BlockSpec(memory_space=pl.ANY)] * 4,
        out_specs=pl.BlockSpec(memory_space=pltpu.VMEM),
        scratch_shapes=[
            pltpu.VMEM((n_super, R, width), BF16),
            pltpu.VMEM((blocks, width, nb), BF16),
            pltpu.VMEM((blocks, width, nb), BF16),
            pltpu.VMEM((NJ, 2 * units, cw), BF16),
            pltpu.VMEM((n_super, R, 2 * units), BF16),
            pltpu.VMEM((n, R, cw), F32),
            one, one, one, one, one, two, two, two, cross, cross,
            dma((n_super + 2 * blocks + NJ,)), dma((NJ,)), dma((NJ,)), dma((n,)), dma((n,)),
            *[dma((n, n1))] * 10,
            *[dma((n, n2))] * 3, *[dma((n,))] * 4, *[dma((n, n2))] * 3,
            dma((n,)), dma((n,)),
        ],
        compiler_params=pltpu.CompilerParams(
            collective_id=0, has_side_effects=True, vmem_limit_bytes=52 * 1024 * 1024
        ),
    )(x, w_gate, w_up, w_down)


def solution(mesh):
    return jax.shard_map(
        block,
        mesh=mesh,
        in_specs=(P("dp", None), P(None, "tp"), P(None, "tp"), P("tp", None)),
        out_specs=P("dp", None),
        check_vma=False,
    )
```

time: 112 us -> 108 us (0.964)
  Pallas kernels: 108 us -> 104 us
    pallas_call x1, Pallas kernels: 108 us -> 104 us  [block(): pl.pallas_call(kernel, out_shape=pltpu.VMEM((rows, width), BF16), in_spec...]
where the time goes in v2:
time: 108 us
  Pallas kernels  104 us (96%)
  local copies, waits for them, and re-layouts  3.4 us (3%)
    pallas_call x1, Pallas kernels, block(): pl.pallas_call(kernel, out_shape=pltpu.VMEM((rows, width), BF16), in_spec...  104 us
    unnamed x1, local copies, waits for them, and re-layouts  3.4 us

profile of v2, /device:TPU:0, one launch (start us, length us, event | category | flops | bytes accessed | tf_op | source)
XLA Modules:
  0.0 107.7 jit_solution(16367810065677567220)
XLA Ops:
  0.0 104.3 %shard_map.46 = bf16[2048,2048]{1,0:T(8,128)(2,1)S(1)} custom-call(bf16[2048,2048]{1,0:T(8,128)(2,1)} %x_hbm.1, bf16[2048,1024]{1,0:T(8,128)(2,1)} %wg_hbm.1, bf16[2048,1024]{1,0:T(8,128)(2,1)} %wu_hbm.1, bf16[1024,2048]{1,0:T(8,128)(2,1)} %wd_hbm.1), custom_call_target="tpu_custom_call" | custom-call | tf_op jit(solution)/shard_map/pallas_call | solution.py:413
  104.3 3.4 %copy.6 = bf16[2048,2048]{1,0:T(8,128)(2,1)} copy(bf16[2048,2048]{1,0:T(8,128)(2,1)S(1)} %shard_map.46) | data formatting | bytes 16777216

commit v3 on v2

--- a/solution.py
+++ b/solution.py
@@ -10,7 +10,7 @@
 F32, BF16 = jnp.float32, jnp.bfloat16
 
 R = 256
-R1, R2 = 192, 64
+R1, R2 = 160, 96
 NJ = 2
 ROOT1 = (0, 3)
 ROOT2 = (0, 3, 1, 2)

time: 108 us -> 112 us (1.037)
  Pallas kernels: 104 us -> 109 us
    pallas_call x1, Pallas kernels: 104 us -> 109 us  [block(): pl.pallas_call(kernel, out_shape=pltpu.VMEM((rows, width), BF16), in_spec...]
where the time goes in v3:
time: 112 us
  Pallas kernels  109 us (97%)
  local copies, waits for them, and re-layouts  3.4 us (3%)
    pallas_call x1, Pallas kernels, block(): pl.pallas_call(kernel, out_shape=pltpu.VMEM((rows, width), BF16), in_spec...  109 us
    unnamed x1, local copies, waits for them, and re-layouts  3.4 us

profile of v3, /device:TPU:0, one launch (start us, length us, event | category | flops | bytes accessed | tf_op | source)
XLA Modules:
  0.0 112.1 jit_solution(3228114439511814601)
XLA Ops:
  0.0 108.7 %shard_map.46 = bf16[2048,2048]{1,0:T(8,128)(2,1)S(1)} custom-call(bf16[2048,2048]{1,0:T(8,128)(2,1)} %x_hbm.1, bf16[2048,1024]{1,0:T(8,128)(2,1)} %wg_hbm.1, bf16[2048,1024]{1,0:T(8,128)(2,1)} %wu_hbm.1, bf16[1024,2048]{1,0:T(8,128)(2,1)} %wd_hbm.1), custom_call_target="tpu_custom_call" | custom-call | tf_op jit(solution)/shard_map/pallas_call | solution.py:413
  108.7 3.4 %copy.6 = bf16[2048,2048]{1,0:T(8,128)(2,1)} copy(bf16[2048,2048]{1,0:T(8,128)(2,1)S(1)} %shard_map.46) | data formatting | bytes 16777216

commit v4 on v2

--- a/solution.py
+++ b/solution.py
@@ -14,7 +14,7 @@
 NJ = 2
 ROOT1 = (0, 3)
 ROOT2 = (0, 3, 1, 2)
-M1, M2 = 1, 1
+M1, M2 = 2, 4
 NZ = 4
 HY, HZ, HX, HB, EB, HF = 2, 2, 2, 2, 1, 0
 

time: 108 us -> 107 us (level)
    pallas_call x1, Pallas kernels: 104 us -> 103 us  [block(): pl.pallas_call(kernel, out_shape=pltpu.VMEM((rows, width), BF16), in_spec...]
where the time goes in v4:
time: 107 us; the launch traced here: 106 us
  Pallas kernels  103 us (96%)
  local copies, waits for them, and re-layouts  3.4 us (3%)
    pallas_call x1, Pallas kernels, block(): pl.pallas_call(kernel, out_shape=pltpu.VMEM((rows, width), BF16), in_spec...  103 us
    unnamed x1, local copies, waits for them, and re-layouts  3.4 us

profile of v4, /device:TPU:0, one launch (start us, length us, event | category | flops | bytes accessed | tf_op | source)
XLA Modules:
  0.0 106.4 jit_solution(4884575779105103362)
XLA Ops:
  0.0 103.0 %shard_map.46 = bf16[2048,2048]{1,0:T(8,128)(2,1)S(1)} custom-call(bf16[2048,2048]{1,0:T(8,128)(2,1)} %x_hbm.1, bf16[2048,1024]{1,0:T(8,128)(2,1)} %wg_hbm.1, bf16[2048,1024]{1,0:T(8,128)(2,1)} %wu_hbm.1, bf16[1024,2048]{1,0:T(8,128)(2,1)} %wd_hbm.1), custom_call_target="tpu_custom_call" | custom-call | tf_op jit(solution)/shard_map/pallas_call | solution.py:413
  103.0 3.4 %copy.6 = bf16[2048,2048]{1,0:T(8,128)(2,1)} copy(bf16[2048,2048]{1,0:T(8,128)(2,1)S(1)} %shard_map.46) | data formatting | bytes 16777216

commit v5 on v4

--- a/solution.py
+++ b/solution.py
@@ -237,10 +237,10 @@
 
         @pl.when((it >= NJ) & (it < n))
         def _():
+            down_wait(it - NJ)
             gate_up_wait(it)
-            down_wait(it - NJ)
+            down(it - NJ)
             gate_up(it)
-            down(it - NJ)
             hid_msg(it).start()
             down_send(it - NJ)
 
@@ -256,24 +256,48 @@
     def guarded(c, f, p=0, m=1):
         pl.when((c >= 0) & (c < n) & active(c, p, m))(lambda: f(c))
 
-    def chain(c, k, acc, lbuf, rbuf, sbuf, msg, root):
-        @pl.when((z >= 1) & (z <= k))
-        def _():
+    def chain(c, k, base, lbuf, rbuf, sbuf, msg, root):
+        if k > 0:
+
+            @pl.when(z == 0)
+            def _():
+                sbuf[...] = base().astype(BF16)
+                msg(True).start()
+
+        if k < NZ - 1:
+
+            @pl.when(z == NZ - 1)
+            def _():
+                sbuf[...] = base().astype(BF16)
+                msg(False).start()
+
+        if k > 1:
+
+            @pl.when((z > 0) & (z < k))
+            def _():
+                msg(True).wait_recv()
+                sbuf[...] = (base() + lbuf[...].astype(F32)).astype(BF16)
+                msg(True).start()
+
+        if k < NZ - 2:
+
+            @pl.when((z < NZ - 1) & (z > k))
+            def _():
+                msg(False).wait_recv()
+                sbuf[...] = (base() + rbuf[...].astype(F32)).astype(BF16)
+                msg(False).start()
+
+        pl.when(z == k)(root)
+
+    def arrived(k, lbuf, rbuf, msg):
+        total = 0.0
+        if k > 0:
             msg(True).wait_recv()
-            acc[...] += lbuf[...].astype(F32)
-
-        @pl.when((z <= NZ - 2) & (z >= k))
-        def _():
+            total = lbuf[...].astype(F32)
+        if k < NZ - 1:
             msg(False).wait_recv()
-            acc[...] += rbuf[...].astype(F32)
-
-        @pl.when(z != k)
-        def _():
-            sbuf[...] = acc[...].astype(BF16)
-            pl.when(z < k)(lambda: msg(True).start())
-            pl.when(z > k)(lambda: msg(False).start())
-
-        pl.when(z == k)(root)
+            total = total + rbuf[...].astype(F32)
+        return total
 
     def spread(k, msg):
         if k < NZ - 1:
@@ -284,16 +308,22 @@
     def reduce1(c, p):
         k = ROOT1[p]
         i = p // M1
-        acc = part1(c, yy, p)
+        bufs = rl1.at[c, i], rr1.at[c, i]
         m_y1(c, p).wait_recv()
-        acc[...] += ry1[c, i].astype(F32)
+
+        def base():
+            return part1(c, yy, p)[...] + ry1[c, i].astype(F32)
+
+        def msg(to_right):
+            return m_z1(c, p, to_right)
 
         def root():
-            y1_place(c, yy, p)[...] = acc[...].astype(BF16)
+            more = arrived(k, *bufs, msg)
+            y1_place(c, yy, p)[...] = (base() + more).astype(BF16)
             spread(k, lambda to_right: m_b1(c, p, to_right))
             m_a1(c, p, yy).start()
 
-        chain(c, k, acc, rl1.at[c, i], rr1.at[c, i], sz1.at[c, i], lambda to_right: m_z1(c, p, to_right), root)
+        chain(c, k, base, *bufs, sz1.at[c, i], msg, root)
 
     def bcast1(c, p):
         k = ROOT1[p]
@@ -307,21 +337,32 @@
     def reduce2(c, q):
         k = ROOT2[q]
         i = q // M2
-        acc = part2(c, q)
+        bufs = rl2.at[c, i], rr2.at[c, i]
+
+        def base():
+            return part2(c, q)[...]
+
+        def msg(to_right):
+            return m_z2(c, q, to_right)
 
         def root():
             @pl.when(jnp.logical_not(y_root(c, q)))
             def _():
-                sy2[c] = acc[...].astype(BF16)
+                more = arrived(k, *bufs, msg)
+                sy2[c] = (base() + more).astype(BF16)
                 m_y2(c, q).start()
 
-        chain(c, k, acc, rl2.at[c, i], rr2.at[c, i], sz2.at[c, i], lambda to_right: m_z2(c, q, to_right), root)
+        chain(c, k, base, *bufs, sz2.at[c, i], msg, root)
 
     def cross2(c, q):
-        @pl.when((z == ROOT2[q]) & y_root(c, q))
-        def _():
+        k = ROOT2[q]
+        i = q // M2
+
+        @pl.when((z == k) & y_root(c, q))
+        def _():
+            more = arrived(k, rl2.at[c, i], rr2.at[c, i], lambda to_right: m_z2(c, q, to_right))
             m_y2(c, q).wait_recv()
-            y2_place(c, q)[...] = (part2(c, q)[...] + ry2[c].astype(F32)).astype(BF16)
+            y2_place(c, q)[...] = (part2(c, q)[...] + more + ry2[c].astype(F32)).astype(BF16)
             m_a2(c, q).start()
 
     def bcast2(c, q):

time: 107 us -> 105 us (0.981)
  Pallas kernels: 103 us -> 101 us
    pallas_call x1, Pallas kernels: 103 us -> 101 us  [block(): pl.pallas_call(kernel, out_shape=pltpu.VMEM((rows, width), BF16), in_spec...]
where the time goes in v5:
time: 105 us
  Pallas kernels  101 us (96%)
  local copies, waits for them, and re-layouts  3.4 us (3%)
    pallas_call x1, Pallas kernels, block(): pl.pallas_call(kernel, out_shape=pltpu.VMEM((rows, width), BF16), in_spec...  101 us
    unnamed x1, local copies, waits for them, and re-layouts  3.4 us

profile of v5, /device:TPU:0, one launch (start us, length us, event | category | flops | bytes accessed | tf_op | source)
XLA Modules:
  0.0 104.7 jit_solution(8696281714102039334)
XLA Ops:
  0.0 101.3 %shard_map.46 = bf16[2048,2048]{1,0:T(8,128)(2,1)S(1)} custom-call(bf16[2048,2048]{1,0:T(8,128)(2,1)} %x_hbm.1, bf16[2048,1024]{1,0:T(8,128)(2,1)} %wg_hbm.1, bf16[2048,1024]{1,0:T(8,128)(2,1)} %wu_hbm.1, bf16[1024,2048]{1,0:T(8,128)(2,1)} %wd_hbm.1), custom_call_target="tpu_custom_call" | custom-call | tf_op jit(solution)/shard_map/pallas_call | solution.py:454
  101.3 3.4 %copy.6 = bf16[2048,2048]{1,0:T(8,128)(2,1)} copy(bf16[2048,2048]{1,0:T(8,128)(2,1)S(1)} %shard_map.46) | data formatting | bytes 16777216

commit v6 on v5

--- a/solution.py
+++ b/solution.py
@@ -10,13 +10,13 @@
 F32, BF16 = jnp.float32, jnp.bfloat16
 
 R = 256
-R1, R2 = 192, 64
+R1, R2 = 208, 48
 NJ = 2
 ROOT1 = (0, 3)
-ROOT2 = (0, 3, 1, 2)
-M1, M2 = 2, 4
+ROOT2 = (0, 2, 1, 3)
+M1, M2 = 1, 4
 NZ = 4
-HY, HZ, HX, HB, EB, HF = 2, 2, 2, 2, 1, 0
+HY, HZ, HX, HB, EB, HF = 2, 2, 3, 3, 0, 1
 
 
 def _far(k):

time: 105 us -> 104 us (level)
  no operation moved by 1% of the time
where the time goes in v6:
time: 104 us
  Pallas kernels  101 us (97%)
  local copies, waits for them, and re-layouts  3.4 us (3%)
    pallas_call x1, Pallas kernels, block(): pl.pallas_call(kernel, out_shape=pltpu.VMEM((rows, width), BF16), in_spec...  101 us
    unnamed x1, local copies, waits for them, and re-layouts  3.4 us

profile of v6, /device:TPU:0, one launch (start us, length us, event | category | flops | bytes accessed | tf_op | source)
XLA Modules:
  0.0 104.3 jit_solution(7096453753349719851)
XLA Ops:
  0.0 100.9 %shard_map.46 = bf16[2048,2048]{1,0:T(8,128)(2,1)S(1)} custom-call(bf16[2048,2048]{1,0:T(8,128)(2,1)} %x_hbm.1, bf16[2048,1024]{1,0:T(8,128)(2,1)} %wg_hbm.1, bf16[2048,1024]{1,0:T(8,128)(2,1)} %wu_hbm.1, bf16[1024,2048]{1,0:T(8,128)(2,1)} %wd_hbm.1), custom_call_target="tpu_custom_call" | custom-call | tf_op jit(solution)/shard_map/pallas_call | solution.py:454
  100.9 3.4 %copy.6 = bf16[2048,2048]{1,0:T(8,128)(2,1)} copy(bf16[2048,2048]{1,0:T(8,128)(2,1)S(1)} %shard_map.46) | data formatting | bytes 16777216

commit v7 on v5

--- a/solution.py
+++ b/solution.py
@@ -12,11 +12,12 @@
 R = 256
 R1, R2 = 192, 64
 NJ = 2
-ROOT1 = (0, 3)
-ROOT2 = (0, 3, 1, 2)
-M1, M2 = 2, 4
+ROOT2 = (0, 1, 2, 3)
+M2 = 1
 NZ = 4
-HY, HZ, HX, HB, EB, HF = 2, 2, 2, 2, 1, 0
+HY, HC, HE, HO, HF = 2, 2, 2, 2, 1
+HZ, HX, HB, E2 = 1, 3, 3, 1
+ORDER = "zscxeob"
 
 
 def _far(k):
@@ -30,11 +31,10 @@
 def kernel(
     x_hbm, wg_hbm, wu_hbm, wd_hbm, y,
     x, wg, wu, wd, hid, part,
-    sy1, ry1, sz1, rl1, rr1, sz2, rl2, rr2, sy2, ry2,
+    sy1, ry1, s1, r_in, r_ex, s2, rl2, rr2, ry2,
     in_sem, wd_s, wd_r, hid_s, hid_r,
-    y1_s, y1_r, z1_s, l1_r, r1_r, bl1_s, br1_s, b1_r, a1_s, a1_r,
-    z2_s, l2_r, r2_r, y2_s, y2_r, a2_s, a2_r, bl2_s, br2_s, b2_r,
-    df_s, df_r,
+    y1_s, y1_r, z1_s, in_r, ex_r, o1_s, o1_r, a1_s, a1_r, y2_s, y2_r, df_s, df_r,
+    z2_s, l2_r, r2_r, bl2_s, br2_s, b2_r,
 ):
     rows, width = y.shape
     n_super = rows // R
@@ -45,7 +45,7 @@
     uh = units // NJ
     nb = min(256, uh)
     blocks = units // nb
-    w1 = cw // 2 * M1 // len(ROOT1)
+    w1 = cw // 2
     w2 = cw * M2 // len(ROOT2)
 
     me = lax.axis_index("tp")
@@ -56,6 +56,10 @@
     ypeer = {"tp": lax.rem(me + 2 * NZ, 4 * NZ)}
     left = {"tp": me - 2}
     right = {"tp": me + 2}
+    outer = (z == 0) | (z == NZ - 1)
+    step_in = jnp.where(z < NZ // 2, 2, -2)
+    inward = {"tp": me + step_in}
+    outward = {"tp": me - step_in}
 
     def load(i, src, dst):
         return pltpu.make_async_copy(src, dst, in_sem.at[i])
@@ -127,56 +131,47 @@
     def col0(c, who):
         return al(who * half + lax.rem(c, NJ) * cw, cw)
 
-    def y1_place(c, h, p):
-        return y.at[pl.ds(row0(c), R1), pl.ds(al(col0(c, core) + h * (cw // 2) + p // M1 * w1, w1), w1)]
+    def y1_place(c, h):
+        return y.at[pl.ds(row0(c), R1), pl.ds(al(col0(c, core) + h * w1, w1), w1)]
 
     def y2_place(c, q):
         return y.at[pl.ds(al(row0(c) + R1, 16), R2), pl.ds(al(col0(c, core) + q // M2 * w2, w2), w2)]
 
-    def part1(c, h, p):
-        return part.at[c, pl.ds(0, R1), pl.ds(al(h * (cw // 2) + p // M1 * w1, w1), w1)]
+    def part1(c, h):
+        return part.at[c, pl.ds(0, R1), pl.ds(al(h * w1, w1), w1)]
 
     def part2(c, q):
         return part.at[c, pl.ds(R1, R2), pl.ds(q // M2 * w2, w2)]
 
-    def m_y1(c, p):
-        i = p // M1
-        return remote(sy1.at[c, i], ry1.at[c, i], y1_s.at[c, i], y1_r.at[c, i], ypeer)
-
-    def m_z1(c, p, to_right):
-        i = p // M1
-        dst, sem = (rl1, l1_r) if to_right else (rr1, r1_r)
-        return remote(sz1.at[c, i], dst.at[c, i], z1_s.at[c, i], sem.at[c, i], right if to_right else left)
-
-    def m_b1(c, p, to_right):
-        i = p // M1
-        place = y1_place(c, yy, p)
-        return remote(place, place, (br1_s if to_right else bl1_s).at[c, i], b1_r.at[c, i], right if to_right else left)
-
-    def m_a1(c, p, h):
-        i = p // M1
-        place = y1_place(c, h, p)
-        return remote(place, place, a1_s.at[c, i], a1_r.at[c, i], ypeer)
+    def m_y1(c):
+        return remote(sy1.at[c], ry1.at[c], y1_s.at[c], y1_r.at[c], ypeer)
+
+    def m_in(c):
+        return remote(s1.at[c], r_in.at[c], z1_s.at[c], in_r.at[c], inward)
+
+    def m_ex(c):
+        return remote(s1.at[c], r_ex.at[c], z1_s.at[c], ex_r.at[c], inward)
+
+    def m_o1(c):
+        place = y1_place(c, yy)
+        return remote(place, place, o1_s.at[c], o1_r.at[c], outward)
+
+    def m_a1(c, h):
+        place = y1_place(c, h)
+        return remote(place, place, a1_s.at[c], a1_r.at[c], ypeer)
 
     def m_z2(c, q, to_right):
         i = q // M2
         dst, sem = (rl2, l2_r) if to_right else (rr2, r2_r)
-        return remote(sz2.at[c, i], dst.at[c, i], z2_s.at[c, i], sem.at[c, i], right if to_right else left)
+        return remote(s2.at[c, i], dst.at[c, i], z2_s.at[c, i], sem.at[c, i], right if to_right else left)
 
     def m_y2(c, q):
-        return remote(sy2.at[c], ry2.at[c], y2_s.at[c], y2_r.at[c], ypeer)
-
-    def m_a2(c, q):
-        place = y2_place(c, q)
-        return remote(place, place, a2_s.at[c], a2_r.at[c], ypeer)
+        return remote(s2.at[c, q // M2], ry2.at[c], y2_s.at[c], y2_r.at[c], ypeer)
 
     def m_b2(c, q, to_right):
         i = q // M2
         place = y2_place(c, q)
         return remote(place, place, (br2_s if to_right else bl2_s).at[c, i], b2_r.at[c, i], right if to_right else left)
-
-    def y_root(c, q):
-        return lax.rem(lax.div(c, M2) + q // 2, 2) == yy
 
     def m_df(c, who):
         place = y.at[pl.ds(row0(c), R), pl.ds(col0(c, who), cw)]
@@ -219,12 +214,8 @@
             part[c, :, cols] = jnp.dot(hid[s], wd[j, :, cols], preferred_element_type=F32)
 
     def down_send(c):
-        for p in range(len(ROOT1)):
-
-            @pl.when(active(c, p, M1))
-            def _():
-                sy1[c, p // M1] = part1(c, 1 - yy, p)[...].astype(BF16)
-                m_y1(c, p).start()
+        sy1[c] = part1(c, 1 - yy)[...].astype(BF16)
+        m_y1(c).start()
 
     def compute(it):
         for j in range(NJ):
@@ -305,34 +296,26 @@
         if k > 0:
             pl.when((z <= k) & (z > 0))(lambda: msg(False).start())
 
-    def reduce1(c, p):
-        k = ROOT1[p]
-        i = p // M1
-        bufs = rl1.at[c, i], rr1.at[c, i]
-        m_y1(c, p).wait_recv()
-
-        def base():
-            return part1(c, yy, p)[...] + ry1[c, i].astype(F32)
-
-        def msg(to_right):
-            return m_z1(c, p, to_right)
-
-        def root():
-            more = arrived(k, *bufs, msg)
-            y1_place(c, yy, p)[...] = (base() + more).astype(BF16)
-            spread(k, lambda to_right: m_b1(c, p, to_right))
-            m_a1(c, p, yy).start()
-
-        chain(c, k, base, *bufs, sz1.at[c, i], msg, root)
-
-    def bcast1(c, p):
-        k = ROOT1[p]
-
-        @pl.when(z != k)
-        def _():
-            m_b1(c, p, True).wait_recv()
-            spread(k, lambda to_right: m_b1(c, p, to_right))
-            m_a1(c, p, yy).start()
+    def outer_in(c):
+        m_y1(c).wait_recv()
+        s1[c] = (part1(c, yy)[...] + ry1[c].astype(F32)).astype(BF16)
+        m_in(c).start()
+
+    def centre_sum(c):
+        m_y1(c).wait_recv()
+        m_in(c).wait_recv()
+        s1[c] = (part1(c, yy)[...] + ry1[c].astype(F32) + r_in[c].astype(F32)).astype(BF16)
+        m_ex(c).start()
+
+    def centre_out(c):
+        m_ex(c).wait_recv()
+        y1_place(c, yy)[...] = (s1[c].astype(F32) + r_ex[c].astype(F32)).astype(BF16)
+        m_o1(c).start()
+        m_a1(c, yy).start()
+
+    def outer_out(c):
+        m_o1(c).wait_recv()
+        m_a1(c, yy).start()
 
     def reduce2(c, q):
         k = ROOT2[q]
@@ -346,56 +329,67 @@
             return m_z2(c, q, to_right)
 
         def root():
-            @pl.when(jnp.logical_not(y_root(c, q)))
-            def _():
-                more = arrived(k, *bufs, msg)
-                sy2[c] = (base() + more).astype(BF16)
-                m_y2(c, q).start()
-
-        chain(c, k, base, *bufs, sz2.at[c, i], msg, root)
+            more = arrived(k, *bufs, msg)
+            s2[c, i] = (base() + more).astype(BF16)
+            m_y2(c, q).start()
+
+        chain(c, k, base, *bufs, s2.at[c, i], msg, root)
 
     def cross2(c, q):
         k = ROOT2[q]
-        i = q // M2
-
-        @pl.when((z == k) & y_root(c, q))
-        def _():
-            more = arrived(k, rl2.at[c, i], rr2.at[c, i], lambda to_right: m_z2(c, q, to_right))
+
+        @pl.when(z == k)
+        def _():
             m_y2(c, q).wait_recv()
-            y2_place(c, q)[...] = (part2(c, q)[...] + more + ry2[c].astype(F32)).astype(BF16)
-            m_a2(c, q).start()
+            y2_place(c, q)[...] = (s2[c, q // M2].astype(F32) + ry2[c].astype(F32)).astype(BF16)
+            spread(k, lambda to_right: m_b2(c, q, to_right))
 
     def bcast2(c, q):
         k = ROOT2[q]
-        pl.when((z == k) & jnp.logical_not(y_root(c, q)))(lambda: m_a2(c, q).wait_recv())
-        pl.when(z != k)(lambda: m_b2(c, q, True).wait_recv())
-        spread(k, lambda to_right: m_b2(c, q, to_right))
+
+        @pl.when(z != k)
+        def _():
+            m_b2(c, q, True).wait_recv()
+            spread(k, lambda to_right: m_b2(c, q, to_right))
 
     def finish(c):
-        for p in range(len(ROOT1)):
-            pl.when(active(c, p, M1))(lambda: m_a1(c, p, 1 - yy).wait_recv())
+        m_a1(c, 1 - yy).wait_recv()
         m_df(c, core).start()
 
     def dist(k):
         return jnp.where(z < k, k - z, z - k)
 
-    last = max(
-        [NJ + HY + EB + HF + (HZ + HB) * _far(k) for k in ROOT1]
-        + [NJ + 2 * HX + EB + (HZ + HB) * _far(k) for k in ROOT2]
-    )
+    def when_in(c, cond, f):
+        pl.when((c >= 0) & (c < n) & cond)(lambda: f(c))
+
+    at_in = NJ + HY
+    at_sum = at_in + HC
+    at_out = at_sum + HE
+    at_end = at_out + HO
+    last = max([at_end + HF] + [NJ + HX + E2 + (HZ + HB) * _far(k) for k in ROOT2])
+    centre = jnp.logical_not(outer)
+
+    def second(it, lag, f):
+        for q, k in enumerate(ROOT2):
+            guarded(it - lag(k), functools.partial(f, q=q), q, M2)
 
     def step(it, carry):
         compute(it)
-        for p, k in enumerate(ROOT1):
-            guarded(it - (NJ + HY) - HZ * _hops(z, k), functools.partial(reduce1, p=p), p, M1)
-        for q, k in enumerate(ROOT2):
-            guarded(it - NJ - HZ * _hops(z, k), functools.partial(reduce2, q=q), q, M2)
-        for q, k in enumerate(ROOT2):
-            guarded(it - (NJ + HX) - HZ * _far(k), functools.partial(cross2, q=q), q, M2)
-        for p, k in enumerate(ROOT1):
-            guarded(it - (NJ + HY + EB) - HZ * _far(k) - HB * dist(k), functools.partial(bcast1, p=p), p, M1)
-        for q, k in enumerate(ROOT2):
-            guarded(it - (NJ + 2 * HX + EB) - HZ * _far(k) - HB * dist(k), functools.partial(bcast2, q=q), q, M2)
+        for name in ORDER:
+            if name == "s":
+                when_in(it - at_in, outer, outer_in)
+            if name == "c":
+                when_in(it - at_sum, centre, centre_sum)
+            if name == "e":
+                when_in(it - at_out, centre, centre_out)
+            if name == "o":
+                when_in(it - at_end, outer, outer_out)
+            if name == "z":
+                second(it, lambda k: NJ + HZ * _hops(z, k), reduce2)
+            if name == "x":
+                second(it, lambda k: NJ + HX + HZ * _far(k), cross2)
+            if name == "b":
+                second(it, lambda k: NJ + HX + E2 + HZ * _far(k) + HB * dist(k), bcast2)
         guarded(it - last, finish)
         return carry
 
@@ -406,25 +400,16 @@
 
     def drain(c, carry):
         hid_msg(c).wait_send()
-        for p, k in enumerate(ROOT1):
-
-            @pl.when(active(c, p, M1))
-            def _():
-                m_y1(c, p).wait_send()
-                pl.when(z != k)(lambda: m_z1(c, p, True).wait_send())
-                if k < NZ - 1:
-                    pl.when((z >= k) & (z < NZ - 1))(lambda: m_b1(c, p, True).wait_send())
-                if k > 0:
-                    pl.when((z <= k) & (z > 0))(lambda: m_b1(c, p, False).wait_send())
-                m_a1(c, p, yy).wait_send()
-
+        m_y1(c).wait_send()
+        m_in(c).wait_send()
+        pl.when(centre)(lambda: m_o1(c).wait_send())
+        m_a1(c, yy).wait_send()
         for q, k in enumerate(ROOT2):
 
             @pl.when(active(c, q, M2))
             def _():
                 pl.when(z != k)(lambda: m_z2(c, q, True).wait_send())
-                pl.when((z == k) & jnp.logical_not(y_root(c, q)))(lambda: m_y2(c, q).wait_send())
-                pl.when((z == k) & y_root(c, q))(lambda: m_a2(c, q).wait_send())
+                pl.when(z == k)(lambda: m_y2(c, q).wait_send())
                 if k < NZ - 1:
                     pl.when((z >= k) & (z < NZ - 1))(lambda: m_b2(c, q, True).wait_send())
                 if k > 0:
@@ -443,12 +428,12 @@
     n_super = rows // R
     n = NJ * n_super
     cw = width // 2 // NJ
-    n1, n2 = len(ROOT1) // M1, len(ROOT2) // M2
-    w1, w2 = cw // 2 // n1, cw // n2
+    n2 = len(ROOT2) // M2
+    w1, w2 = cw // 2, cw // n2
     nb = min(256, units // NJ)
     blocks = units // nb
     dma = pltpu.SemaphoreType.DMA
-    one = pltpu.VMEM((n, n1, R1, w1), BF16)
+    one = pltpu.VMEM((n, R1, w1), BF16)
     two = pltpu.VMEM((n, n2, R2, w2), BF16)
     cross = pltpu.VMEM((n, R2, w2), BF16)
     return pl.pallas_call(
@@ -463,11 +448,10 @@
             pltpu.VMEM((NJ, 2 * units, cw), BF16),
             pltpu.VMEM((n_super, R, 2 * units), BF16),
             pltpu.VMEM((n, R, cw), F32),
-            one, one, one, one, one, two, two, two, cross, cross,
+            one, one, one, one, one, two, two, two, cross,
             dma((n_super + 2 * blocks + NJ,)), dma((NJ,)), dma((NJ,)), dma((n,)), dma((n,)),
-            *[dma((n, n1))] * 10,
-            *[dma((n, n2))] * 3, *[dma((n,))] * 4, *[dma((n, n2))] * 3,
-            dma((n,)), dma((n,)),
+            *[dma((n,))] * 13,
+            *[dma((n, n2))] * 6,
         ],
         compiler_params=pltpu.CompilerParams(
             collective_id=0, has_side_effects=True, vmem_limit_bytes=52 * 1024 * 1024

time: 105 us -> 103 us (0.981)
  Pallas kernels: 101 us -> 99.2 us
    pallas_call x1, Pallas kernels: 101 us -> 99.2 us  [block(): pl.pallas_call(kernel, out_shape=pltpu.VMEM((rows, width), BF16), in_spec...]
where the time goes in v7:
time: 103 us
  Pallas kernels  99.2 us (96%)
  local copies, waits for them, and re-layouts  3.4 us (3%)
    pallas_call x1, Pallas kernels, block(): pl.pallas_call(kernel, out_shape=pltpu.VMEM((rows, width), BF16), in_spec...  99.2 us
    unnamed x1, local copies, waits for them, and re-layouts  3.4 us

profile of v7, /device:TPU:0, one launch (start us, length us, event | category | flops | bytes accessed | tf_op | source)
XLA Modules:
  0.0 102.6 jit_solution(5198930825200310103)
XLA Ops:
  0.0 99.2 %shard_map.46 = bf16[2048,2048]{1,0:T(8,128)(2,1)S(1)} custom-call(bf16[2048,2048]{1,0:T(8,128)(2,1)} %x_hbm.1, bf16[2048,1024]{1,0:T(8,128)(2,1)} %wg_hbm.1, bf16[2048,1024]{1,0:T(8,128)(2,1)} %wu_hbm.1, bf16[1024,2048]{1,0:T(8,128)(2,1)} %wd_hbm.1), custom_call_target="tpu_custom_call" | custom-call | tf_op jit(solution)/shard_map/pallas_call | solution.py:439
  99.2 3.4 %copy.6 = bf16[2048,2048]{1,0:T(8,128)(2,1)} copy(bf16[2048,2048]{1,0:T(8,128)(2,1)S(1)} %shard_map.46) | data formatting | bytes 16777216

commit v8 on v7

--- a/solution.py
+++ b/solution.py
@@ -12,12 +12,12 @@
 R = 256
 R1, R2 = 192, 64
 NJ = 2
-ROOT2 = (0, 1, 2, 3)
-M2 = 1
+ROOT2 = (0, 3, 1, 2)
+M2 = 4
 NZ = 4
-HY, HC, HE, HO, HF = 2, 2, 2, 2, 1
-HZ, HX, HB, E2 = 1, 3, 3, 1
-ORDER = "zscxeob"
+HY, HC, HE, HO, HF = 3, 2, 2, 2, 1
+HZ, HX, HB, E2 = 2, 3, 2, 0
+ORDER = "sczexob"
 
 
 def _far(k):

time: 103 us -> 98.8 us (0.959)
  Pallas kernels: 99.2 us -> 95.2 us
    pallas_call x1, Pallas kernels: 99.2 us -> 95.2 us  [block(): pl.pallas_call(kernel, out_shape=pltpu.VMEM((rows, width), BF16), in_spec...]
where the time goes in v8:
time: 98.8 us; the launch traced here: 98.7 us
  Pallas kernels  95.2 us (96%)
  local copies, waits for them, and re-layouts  3.4 us (3%)
    pallas_call x1, Pallas kernels, block(): pl.pallas_call(kernel, out_shape=pltpu.VMEM((rows, width), BF16), in_spec...  95.2 us
    unnamed x1, local copies, waits for them, and re-layouts  3.4 us

profile of v8, /device:TPU:0, one launch (start us, length us, event | category | flops | bytes accessed | tf_op | source)
XLA Modules:
  0.0 98.7 jit_solution(11211720958826193611)
XLA Ops:
  0.0 95.2 %shard_map.46 = bf16[2048,2048]{1,0:T(8,128)(2,1)S(1)} custom-call(bf16[2048,2048]{1,0:T(8,128)(2,1)} %x_hbm.1, bf16[2048,1024]{1,0:T(8,128)(2,1)} %wg_hbm.1, bf16[2048,1024]{1,0:T(8,128)(2,1)} %wu_hbm.1, bf16[1024,2048]{1,0:T(8,128)(2,1)} %wd_hbm.1), custom_call_target="tpu_custom_call" | custom-call | tf_op jit(solution)/shard_map/pallas_call | solution.py:439
  95.3 3.4 %copy.6 = bf16[2048,2048]{1,0:T(8,128)(2,1)} copy(bf16[2048,2048]{1,0:T(8,128)(2,1)S(1)} %shard_map.46) | data formatting | bytes 16777216

commit v9 on v8

--- a/solution.py
+++ b/solution.py
@@ -415,11 +415,28 @@
                 if k > 0:
                     pl.when((z <= k) & (z > 0))(lambda: m_b2(c, q, False).wait_send())
 
+        return carry
+
+    lax.fori_loop(0, n, drain, 0)
+
+    def drain_rows(c, carry):
         m_df(c, core).wait_send()
         m_df(c, 1 - core).wait_recv()
         return carry
 
-    lax.fori_loop(0, n, drain, 0)
+    lax.fori_loop(0, n, drain_rows, 0)
+
+
+def put_out(y, out, sem):
+    parts = sem.shape[0]
+    rows = y.shape[0] // parts
+    copies = [
+        pltpu.make_async_copy(y.at[pl.ds(i * rows, rows)], out.at[pl.ds(i * rows, rows)], sem.at[i]) for i in range(parts)
+    ]
+    for c in copies:
+        c.start()
+    for c in copies:
+        c.wait()
 
 
 def block(x, w_gate, w_up, w_down):
@@ -436,7 +453,7 @@
     one = pltpu.VMEM((n, R1, w1), BF16)
     two = pltpu.VMEM((n, n2, R2, w2), BF16)
     cross = pltpu.VMEM((n, R2, w2), BF16)
-    return pl.pallas_call(
+    y = pl.pallas_call(
         kernel,
         out_shape=pltpu.VMEM((rows, width), BF16),
         in_specs=[pl.BlockSpec(memory_space=pl.ANY)] * 4,
@@ -457,6 +474,15 @@
             collective_id=0, has_side_effects=True, vmem_limit_bytes=52 * 1024 * 1024
         ),
     )(x, w_gate, w_up, w_down)
+    return pl.pallas_call(
+        put_out,
+        out_shape=jax.ShapeDtypeStruct((rows, width), BF16),
+        in_specs=[pl.BlockSpec(memory_space=pltpu.VMEM)],
+        out_specs=pl.BlockSpec(memory_space=pl.ANY),
+        scratch_shapes=[dma((8,))],
+        name="put_out",
+        compiler_params=pltpu.CompilerParams(vmem_limit_bytes=1024 * 1024),
+    )(y)
 
 
 def solution(mesh):

time: 98.8 us -> 98.8 us (level)
  local copies, waits for them, and re-layouts: 3.4 us -> 0 us
  Pallas kernels: 95.2 us -> 98.6 us
    unnamed x1 -> x0, local copies, waits for them, and re-layouts: 3.4 us -> none
    pallas_call x0 -> x1, Pallas kernels: none -> 3.37 us  [block(): pl.pallas_call(put_out, out_shape=jax.ShapeDtypeStruct((rows, width), BF1...]
where the time goes in v9:
time: 98.8 us; the launch traced here: 98.6 us
  Pallas kernels  98.6 us (100%)
    pallas_call x1, Pallas kernels, block(): pl.pallas_call(kernel, out_shape=pltpu.VMEM((rows, width), BF16), in_spec...  95.2 us
    pallas_call x1, Pallas kernels, block(): pl.pallas_call(put_out, out_shape=jax.ShapeDtypeStruct((rows, width), BF1...  3.37 us

profile of v9, /device:TPU:0, one launch (start us, length us, event | category | flops | bytes accessed | tf_op | source)
XLA Modules:
  0.0 98.6 jit_solution(6874900280400017314)
XLA Ops:
  0.0 95.2 %shard_map.46.y = bf16[2048,2048]{1,0:T(8,128)(2,1)S(1)} custom-call(bf16[2048,2048]{1,0:T(8,128)(2,1)} %x_hbm.1, bf16[2048,1024]{1,0:T(8,128)(2,1)} %wg_hbm.1, bf16[2048,1024]{1,0:T(8,128)(2,1)} %wu_hbm.1, bf16[1024,2048]{1,0:T(8,128)(2,1)} %wd_hbm.1), custom_call_target="tpu_custom_call" | custom-call | tf_op jit(solution)/shard_map/pallas_call | solution.py:456
  95.3 3.4 %put_out.1 = bf16[2048,2048]{1,0:T(8,128)(2,1)} custom-call(bf16[2048,2048]{1,0:T(8,128)(2,1)S(1)} %shard_map.46.y), custom_call_target="tpu_custom_call" | custom-call | tf_op jit(solution)/shard_map/put_out/pallas_call | solution.py:477

commit v10 on v9

--- a/solution.py
+++ b/solution.py
@@ -12,12 +12,12 @@
 R = 256
 R1, R2 = 192, 64
 NJ = 2
-ROOT2 = (0, 3, 1, 2)
+ROOT2 = (0, 3, 2, 1)
 M2 = 4
 NZ = 4
-HY, HC, HE, HO, HF = 3, 2, 2, 2, 1
-HZ, HX, HB, E2 = 2, 3, 2, 0
-ORDER = "sczexob"
+HY, HC, HE, HO, HF = 3, 2, 2, 2, 0
+HZ, HX, HB, E2 = 2, 4, 2, 0
+ORDER = "zsecxob"
 
 
 def _far(k):

time: 98.8 us -> 97.2 us (0.984)
  Pallas kernels: 98.6 us -> 97.1 us
    pallas_call x1, Pallas kernels: 95.2 us -> 93.7 us  [block(): pl.pallas_call(kernel, out_shape=pltpu.VMEM((rows, width), BF16), in_spec...]
where the time goes in v10:
time: 97.2 us; the launch traced here: 97.1 us
  Pallas kernels  97.1 us (100%)
    pallas_call x1, Pallas kernels, block(): pl.pallas_call(kernel, out_shape=pltpu.VMEM((rows, width), BF16), in_spec...  93.7 us
    pallas_call x1, Pallas kernels, block(): pl.pallas_call(put_out, out_shape=jax.ShapeDtypeStruct((rows, width), BF1...  3.37 us

profile of v10, /device:TPU:0, one launch (start us, length us, event | category | flops | bytes accessed | tf_op | source)
XLA Modules:
  0.0 97.1 jit_solution(14912746455866979094)
XLA Ops:
  0.0 93.7 %shard_map.46.y = bf16[2048,2048]{1,0:T(8,128)(2,1)S(1)} custom-call(bf16[2048,2048]{1,0:T(8,128)(2,1)} %x_hbm.1, bf16[2048,1024]{1,0:T(8,128)(2,1)} %wg_hbm.1, bf16[2048,1024]{1,0:T(8,128)(2,1)} %wu_hbm.1, bf16[1024,2048]{1,0:T(8,128)(2,1)} %wd_hbm.1), custom_call_target="tpu_custom_call" | custom-call | tf_op jit(solution)/shard_map/pallas_call | solution.py:456
  93.7 3.4 %put_out.1 = bf16[2048,2048]{1,0:T(8,128)(2,1)} custom-call(bf16[2048,2048]{1,0:T(8,128)(2,1)S(1)} %shard_map.46.y), custom_call_target="tpu_custom_call" | custom-call | tf_op jit(solution)/shard_map/put_out/pallas_call | solution.py:477

commit v11 on v10

--- a/solution.py
+++ b/solution.py
@@ -182,9 +182,9 @@
         def _():
             x_copy(lax.div(it, NJ)).wait()
 
-    def gate_up(it, first=None):
+    def gate_up(it, first=None, part_of=range(uh // nb)):
         s, j = lax.div(it, NJ), lax.rem(it, NJ)
-        for b in range(uh // nb):
+        for b in part_of:
             block = j * (uh // nb) + b
             if first is not None:
                 g_copy(first * (uh // nb) + b).wait()
@@ -226,10 +226,19 @@
                 gate_up(it, first=j)
                 hid_msg(it).start()
 
-        @pl.when((it >= NJ) & (it < n))
-        def _():
+        @pl.when((it >= NJ) & (it < n) & (lax.rem(it, NJ) == 0))
+        def _():
+            gate_up_wait(it)
+            gate_up(it, part_of=range(1))
             down_wait(it - NJ)
-            gate_up_wait(it)
+            down(it - NJ)
+            gate_up(it, part_of=range(1, uh // nb))
+            hid_msg(it).start()
+            down_send(it - NJ)
+
+        @pl.when((it >= NJ) & (it < n) & (lax.rem(it, NJ) != 0))
+        def _():
+            down_wait(it - NJ)
             down(it - NJ)
             gate_up(it)
             hid_msg(it).start()

time: 97.2 us -> 96.7 us (level)
  no operation moved by 1% of the time
where the time goes in v11:
time: 96.7 us; the launch traced here: 96.5 us
  Pallas kernels  96.5 us (100%)
    pallas_call x1, Pallas kernels, block(): pl.pallas_call(kernel, out_shape=pltpu.VMEM((rows, width), BF16), in_spec...  93.1 us
    pallas_call x1, Pallas kernels, block(): pl.pallas_call(put_out, out_shape=jax.ShapeDtypeStruct((rows, width), BF1...  3.37 us

profile of v11, /device:TPU:0, one launch (start us, length us, event | category | flops | bytes accessed | tf_op | source)
XLA Modules:
  0.0 96.5 jit_solution(11700139160596577267)
XLA Ops:
  0.0 93.1 %shard_map.46.y = bf16[2048,2048]{1,0:T(8,128)(2,1)S(1)} custom-call(bf16[2048,2048]{1,0:T(8,128)(2,1)} %x_hbm.1, bf16[2048,1024]{1,0:T(8,128)(2,1)} %wg_hbm.1, bf16[2048,1024]{1,0:T(8,128)(2,1)} %wu_hbm.1, bf16[1024,2048]{1,0:T(8,128)(2,1)} %wd_hbm.1), custom_call_target="tpu_custom_call" | custom-call | tf_op jit(solution)/shard_map/pallas_call | solution.py:465
  93.1 3.4 %put_out.1 = bf16[2048,2048]{1,0:T(8,128)(2,1)} custom-call(bf16[2048,2048]{1,0:T(8,128)(2,1)S(1)} %shard_map.46.y), custom_call_target="tpu_custom_call" | custom-call | tf_op jit(solution)/shard_map/put_out/pallas_call | solution.py:486

commit v12 on v11

--- a/solution.py
+++ b/solution.py
@@ -382,6 +382,23 @@
         for q, k in enumerate(ROOT2):
             guarded(it - lag(k), functools.partial(f, q=q), q, M2)
 
+    def drain(c):
+        hid_msg(c).wait_send()
+        m_y1(c).wait_send()
+        m_in(c).wait_send()
+        pl.when(centre)(lambda: m_o1(c).wait_send())
+        m_a1(c, yy).wait_send()
+        for q, k in enumerate(ROOT2):
+
+            @pl.when(active(c, q, M2))
+            def _():
+                pl.when(z != k)(lambda: m_z2(c, q, True).wait_send())
+                pl.when(z == k)(lambda: m_y2(c, q).wait_send())
+                if k < NZ - 1:
+                    pl.when((z >= k) & (z < NZ - 1))(lambda: m_b2(c, q, True).wait_send())
+                if k > 0:
+                    pl.when((z <= k) & (z > 0))(lambda: m_b2(c, q, False).wait_send())
+
     def step(it, carry):
         compute(it)
         for name in ORDER:
@@ -400,6 +417,7 @@
             if name == "b":
                 second(it, lambda k: NJ + HX + E2 + HZ * _far(k) + HB * dist(k), bcast2)
         guarded(it - last, finish)
+        guarded(it - last - 1, drain)
         return carry
 
     lax.fori_loop(0, n + last, step, 0)
@@ -407,26 +425,7 @@
     for j in range(NJ):
         wd_msg(j).wait_send()
 
-    def drain(c, carry):
-        hid_msg(c).wait_send()
-        m_y1(c).wait_send()
-        m_in(c).wait_send()
-        pl.when(centre)(lambda: m_o1(c).wait_send())
-        m_a1(c, yy).wait_send()
-        for q, k in enumerate(ROOT2):
-
-            @pl.when(active(c, q, M2))
-            def _():
-                pl.when(z != k)(lambda: m_z2(c, q, True).wait_send())
-                pl.when(z == k)(lambda: m_y2(c, q).wait_send())
-                if k < NZ - 1:
-                    pl.when((z >= k) & (z < NZ - 1))(lambda: m_b2(c, q, True).wait_send())
-                if k > 0:
-                    pl.when((z <= k) & (z > 0))(lambda: m_b2(c, q, False).wait_send())
-
-        return carry
-
-    lax.fori_loop(0, n, drain, 0)
+    drain(n - 1)
 
     def drain_rows(c, carry):
         m_df(c, core).wait_send()

time: 96.7 us -> 96.7 us (level)
  no operation moved by 1% of the time
where the time goes in v12:
time: 96.7 us; the launch traced here: 96.6 us
  Pallas kernels  96.6 us (100%)
    pallas_call x1, Pallas kernels, block(): pl.pallas_call(kernel, out_shape=pltpu.VMEM((rows, width), BF16), in_spec...  93.2 us
    pallas_call x1, Pallas kernels, block(): pl.pallas_call(put_out, out_shape=jax.ShapeDtypeStruct((rows, width), BF1...  3.37 us

profile of v12, /device:TPU:0, one launch (start us, length us, event | category | flops | bytes accessed | tf_op | source)
XLA Modules:
  0.0 96.6 jit_solution(7035030370793836319)
XLA Ops:
  0.0 93.2 %shard_map.46.y = bf16[2048,2048]{1,0:T(8,128)(2,1)S(1)} custom-call(bf16[2048,2048]{1,0:T(8,128)(2,1)} %x_hbm.1, bf16[2048,1024]{1,0:T(8,128)(2,1)} %wg_hbm.1, bf16[2048,1024]{1,0:T(8,128)(2,1)} %wu_hbm.1, bf16[1024,2048]{1,0:T(8,128)(2,1)} %wd_hbm.1), custom_call_target="tpu_custom_call" | custom-call | tf_op jit(solution)/shard_map/pallas_call | solution.py:464
  93.2 3.4 %put_out.1 = bf16[2048,2048]{1,0:T(8,128)(2,1)} custom-call(bf16[2048,2048]{1,0:T(8,128)(2,1)S(1)} %shard_map.46.y), custom_call_target="tpu_custom_call" | custom-call | tf_op jit(solution)/shard_map/put_out/pallas_call | solution.py:485

commit v13 on v10

--- a/solution.py
+++ b/solution.py
@@ -30,7 +30,7 @@
 
 def kernel(
     x_hbm, wg_hbm, wu_hbm, wd_hbm, y,
-    x, wg, wu, wd, hid, part,
+    x, wg, wu, wd, hid0, hid1, part,
     sy1, ry1, s1, r_in, r_ex, s2, rl2, rr2, ry2,
     in_sem, wd_s, wd_r, hid_s, hid_r,
     y1_s, y1_r, z1_s, in_r, ex_r, o1_s, o1_r, a1_s, a1_r, y2_s, y2_r, df_s, df_r,
@@ -120,9 +120,11 @@
     for s in range(2, n_super):
         x_copy(s).start()
 
-    def hid_msg(c):
-        s, j = lax.div(c, NJ), lax.rem(c, NJ)
-        place = hid.at[s, :, pl.ds(al(core * units + j * uh, uh), uh)]
+    hid = hid0, hid1
+
+    def hid_msg(c, odd):
+        s, j = lax.div(c, 2 * NJ), lax.rem(c, NJ)
+        place = hid[odd].at[s, :, pl.ds(al(core * units + j * uh, uh), uh)]
         return remote(place, place, hid_s.at[c], hid_r.at[c], peer)
 
     def row0(c):
@@ -182,18 +184,19 @@
         def _():
             x_copy(lax.div(it, NJ)).wait()
 
-    def gate_up(it, first=None):
+    def gate_up(it, odd, first=None, part_of=range(uh // nb)):
         s, j = lax.div(it, NJ), lax.rem(it, NJ)
-        for b in range(uh // nb):
+        for b in part_of:
             block = j * (uh // nb) + b
             if first is not None:
                 g_copy(first * (uh // nb) + b).wait()
                 u_copy(first * (uh // nb) + b).wait()
             gate = jnp.dot(x[s], wg[block], preferred_element_type=F32)
             up = jnp.dot(x[s], wu[block], preferred_element_type=F32)
-            hid[s, :, pl.ds(al(core * units + j * uh + b * nb, nb), nb)] = (jax.nn.gelu(gate) * up).astype(BF16)
-
-    def down_wait(c):
+            cols = pl.ds(al(core * units + j * uh + b * nb, nb), nb)
+            hid[odd][lax.div(s, 2), :, cols] = (jax.nn.gelu(gate) * up).astype(BF16)
+
+    def down_wait(c, odd):
         for j in range(NJ):
 
             @pl.when(c == j)
@@ -204,14 +207,16 @@
         @pl.when(lax.rem(c, NJ) == 0)
         def _():
             for j in range(NJ):
-                hid_msg(c + j).wait_recv()
-
-    def down(c):
-        s, j = lax.div(c, NJ), lax.rem(c, NJ)
-        db = min(256, cw)
-        for b in range(cw // db):
+                hid_msg(c + j, odd).wait_recv()
+
+    def down(c, odd, blocks):
+        s, j = lax.div(c, 2 * NJ), lax.rem(c, NJ)
+        for b in blocks:
             cols = pl.ds(b * db, db)
-            part[c, :, cols] = jnp.dot(hid[s], wd[j, :, cols], preferred_element_type=F32)
+            part[c, :, cols] = jnp.dot(hid[odd][s], wd[j, :, cols], preferred_element_type=F32)
+
+    db = min(256, cw)
+    down_blocks = range(cw // db)
 
     def down_send(c):
         sy1[c] = part1(c, 1 - yy)[...].astype(BF16)
@@ -223,22 +228,35 @@
             @pl.when(it == j)
             def _():
                 gate_up_wait(it)
-                gate_up(it, first=j)
-                hid_msg(it).start()
-
-        @pl.when((it >= NJ) & (it < n))
-        def _():
-            down_wait(it - NJ)
-            gate_up_wait(it)
-            down(it - NJ)
-            gate_up(it)
-            hid_msg(it).start()
-            down_send(it - NJ)
+                gate_up(it, 0, first=j)
+                hid_msg(it, 0).start()
+
+        for odd in range(2):
+            here = (it >= NJ) & (it < n) & (lax.rem(lax.div(it, NJ), 2) == odd)
+
+            @pl.when(here & (lax.rem(it, NJ) == 0))
+            def _():
+                gate_up_wait(it)
+                gate_up(it, odd, part_of=range(1))
+                down_wait(it - NJ, 1 - odd)
+                gate_up(it, odd, part_of=range(1, uh // nb))
+                down(it - NJ, 1 - odd, down_blocks)
+                hid_msg(it, odd).start()
+                down_send(it - NJ)
+
+            @pl.when(here & (lax.rem(it, NJ) != 0))
+            def _():
+                down_wait(it - NJ, 1 - odd)
+                gate_up(it, odd)
+                down(it - NJ, 1 - odd, down_blocks)
+                hid_msg(it, odd).start()
+                down_send(it - NJ)
 
         @pl.when((it >= n) & (it < n + NJ))
         def _():
-            down_wait(it - NJ)
-            down(it - NJ)
+            odd = (n_super - 1) % 2
+            down_wait(it - NJ, odd)
+            down(it - NJ, odd, down_blocks)
             down_send(it - NJ)
 
     def active(c, p, m):
@@ -399,7 +417,8 @@
         wd_msg(j).wait_send()
 
     def drain(c, carry):
-        hid_msg(c).wait_send()
+        for odd in range(2):
+            pl.when(lax.rem(lax.div(c, NJ), 2) == odd)(lambda: hid_msg(c, odd).wait_send())
         m_y1(c).wait_send()
         m_in(c).wait_send()
         pl.when(centre)(lambda: m_o1(c).wait_send())
@@ -463,7 +482,7 @@
             pltpu.VMEM((blocks, width, nb), BF16),
             pltpu.VMEM((blocks, width, nb), BF16),
             pltpu.VMEM((NJ, 2 * units, cw), BF16),
-            pltpu.VMEM((n_super, R, 2 * units), BF16),
+            *[pltpu.VMEM(((n_super + 1) // 2, R, 2 * units), BF16)] * 2,
             pltpu.VMEM((n, R, cw), F32),
             one, one, one, one, one, two, two, two, cross,
             dma((n_super + 2 * blocks + NJ,)), dma((NJ,)), dma((NJ,)), dma((n,)), dma((n,)),

time: 97.2 us -> 96.9 us (level)
  no operation moved by 1% of the time
where the time goes in v13:
time: 96.9 us; the launch traced here: 96.7 us
  Pallas kernels  96.7 us (100%)
    pallas_call x1, Pallas kernels, block(): pl.pallas_call(kernel, out_shape=pltpu.VMEM((rows, width), BF16), in_spec...  93.3 us
    pallas_call x1, Pallas kernels, block(): pl.pallas_call(put_out, out_shape=jax.ShapeDtypeStruct((rows, width), BF1...  3.37 us

profile of v13, /device:TPU:0, one launch (start us, length us, event | category | flops | bytes accessed | tf_op | source)
XLA Modules:
  0.0 96.7 jit_solution(12038761594389594629)
XLA Ops:
  0.0 93.3 %shard_map.46.y = bf16[2048,2048]{1,0:T(8,128)(2,1)S(1)} custom-call(bf16[2048,2048]{1,0:T(8,128)(2,1)} %x_hbm.1, bf16[2048,1024]{1,0:T(8,128)(2,1)} %wg_hbm.1, bf16[2048,1024]{1,0:T(8,128)(2,1)} %wu_hbm.1, bf16[1024,2048]{1,0:T(8,128)(2,1)} %wd_hbm.1), custom_call_target="tpu_custom_call" | custom-call | tf_op jit(solution)/shard_map/pallas_call | solution.py:475
  93.3 3.4 %put_out.1 = bf16[2048,2048]{1,0:T(8,128)(2,1)} custom-call(bf16[2048,2048]{1,0:T(8,128)(2,1)S(1)} %shard_map.46.y), custom_call_target="tpu_custom_call" | custom-call | tf_op jit(solution)/shard_map/put_out/pallas_call | solution.py:496
